TPU v7x, 32 devices: a whole 2x2x4 slice. The times are simulated.
32 devices in a mesh: pair: 2 (over core), dp: 16 (over z, y, x).
Axes of the slice: x: 2, y: 2, z: 4, core: 2. Of those that a mesh axis runs over, the one named last changes fastest.
Arguments:
- inputs: bfloat16 [2, 32, 512, 768], P('pair', 'dp'), may hold values from -6 to 6
- cotangent: bfloat16 [2, 32, 512, 768], P('pair', 'dp'), may hold values from -6 to 6
- span_lengths: int32 [2, 32, 4], P('pair', 'dp'), may hold values from 64 to 320, as said below
- pad_lengths: int32 [2, 32], P('pair', 'dp'), may hold values from 0 to 128, as said below
- pairing: int32 [2, 16, 8], P('pair', 'dp'), may hold values from 0 to 7, as said below
- owner_slot: int32 [108], replicated, may hold values from 0 to 111, as said below
- master: float32 [112, 256, 256], P('dp'), as said below
- first_moment: float32 [112, 256, 256], P('dp'), may hold values from -4 to 4
- second_moment: float32 [112, 256, 256], P('dp'), may hold values from 0.16 to 16
- left_basis: float32 [112, 256, 256], P('dp'), may hold values from -1 to 1
- right_basis: float32 [112, 256, 256], P('dp'), may hold values from -1 to 1
- vector_master: float32 [9216], replicated
- vector_first: float32 [9216], replicated, may hold values from -4 to 4
- vector_second: float32 [9216], replicated, may hold values from 0.16 to 16
Outputs:
- block_output: bfloat16 [2, 32, 512, 768], P('pair', 'dp')
- input_grad: float32 [2, 32, 512, 768], P('pair', 'dp')
- weight_grad: float32 [112, 256, 256], P('dp')
- new_master: float32 [112, 256, 256], P('dp')
- new_first: float32 [112, 256, 256], P('dp')
- new_second: float32 [112, 256, 256], P('dp')
- vector_grad: float32 [9216], replicated
- vector_state: float32 [3, 9216], replicated
Inputs may be any that keep to these rules, and one draw needn't show every extreme that they name: `span_lengths`: each row's spans come first in order and each has 64 tokens or more; the row's padding follows them; some span has exactly 320 tokens. `pad_lengths`: equals 512 minus the sum of the row's span lengths; some row has exactly 128, some row has none. For each dp index, pairing[0] is a permutation of the 8 spans of the partner device and pairing[1] is its inverse; spans are numbered row by row. `owner_slot`: distinct values; slot p belongs to dp index p // 7; every dp index holds at most 7 blocks and some hold exactly 7. `master`: slots that no block uses hold values that take part in no output but their own update.
All inputs are finite; a program needn't handle non-finite values.
Results may differ from a plain program's by a relative error of at most 0.012.
Values may be sent and summed in bfloat16 or wider, within the bound.
A program may use at most 256 MiB of HBM per device.

v0:
```python
import math
import jax
import jax.numpy as jnp
from jax import lax
from jax.sharding import PartitionSpec as P

D = 768
HEADS = 12
FF = 3072
SEGS = 4
STEP = 10
HIGHEST = lax.Precision.HIGHEST
BETA_ONE = 0.9
BETA_TWO = 0.95
ADAM_EPS = 1e-08
LR_MATRIX = 0.1
LR_VECTOR = 1.0
DECAY_RATE = 0.01
NORM_EPS = 1e-12
CLS_SCALE = 0.0625
CLS_WEIGHT = 4.0


def swapped(array, axis, stride):
    return lax.ppermute(array, axis, [(i, i ^ 1 << stride) for i in range(lax.axis_size(axis))])


def layer_norm(values, gain_vector, shift_vector):
    average = jnp.mean(values, axis=-1, keepdims=True)
    centered = values - average
    variance = jnp.mean(centered * centered, axis=-1, keepdims=True)
    return centered * lax.rsqrt(variance + NORM_EPS) * gain_vector + shift_vector


def gelu_exact(values):
    return jax.nn.gelu(values, approximate=False)


def split_vector(vector):
    pieces = [vector[index * D : (index + 1) * D] for index in range(8)]
    return tuple(pieces) + (vector[8 * D : 8 * D + FF],)


def tiled(stack, count_rows, count_cols):
    block_side = stack.shape[-1]
    return (
        stack.reshape(count_rows, count_cols, block_side, block_side)
        .transpose(0, 2, 1, 3)
        .reshape(count_rows * block_side, count_cols * block_side)
    )


def untiled(matrix, block_side):
    count_rows = matrix.shape[0] // block_side
    count_cols = matrix.shape[1] // block_side
    return (
        matrix.reshape(count_rows, block_side, count_cols, block_side)
        .transpose(0, 2, 1, 3)
        .reshape(count_rows * count_cols, block_side, block_side)
    )


def assemble(blocks):
    block_side = blocks.shape[-1]
    row_tiles = D // block_side
    wide_tiles = FF // block_side
    square = row_tiles * row_tiles
    wide_count = row_tiles * wide_tiles
    mats = [
        tiled(blocks[index * square : (index + 1) * square], row_tiles, row_tiles)
        for index in range(4)
    ]
    mats.append(tiled(blocks[4 * square : 4 * square + wide_count], row_tiles, wide_tiles))
    mats.append(
        tiled(blocks[4 * square + wide_count : 4 * square + 2 * wide_count], wide_tiles, row_tiles)
    )
    return tuple(mats)


def disassemble(mats, block_side):
    return jnp.concatenate([untiled(matrix, block_side) for matrix in mats], axis=0)


def soap_update(gradient, weight, moment_one, moment_two, left_basis, right_basis):
    rotated = jnp.matmul(
        jnp.matmul(jnp.swapaxes(left_basis, -1, -2), gradient, precision=HIGHEST),
        right_basis,
        precision=HIGHEST,
    )
    moment_one = BETA_ONE * moment_one + (1.0 - BETA_ONE) * rotated
    moment_two = BETA_TWO * moment_two + (1.0 - BETA_TWO) * rotated * rotated
    direction = (
        moment_one
        / (1.0 - BETA_ONE**STEP)
        / (jnp.sqrt(moment_two / (1.0 - BETA_TWO**STEP)) + ADAM_EPS)
    )
    restored = jnp.matmul(
        jnp.matmul(left_basis, direction, precision=HIGHEST),
        jnp.swapaxes(right_basis, -1, -2),
        precision=HIGHEST,
    )
    return (weight - LR_MATRIX * (restored + DECAY_RATE * weight), moment_one, moment_two)


def adam_update(gradient, weight, moment_one, moment_two):
    moment_one = BETA_ONE * moment_one + (1.0 - BETA_ONE) * gradient
    moment_two = BETA_TWO * moment_two + (1.0 - BETA_TWO) * gradient * gradient
    direction = (
        moment_one
        / (1.0 - BETA_ONE**STEP)
        / (jnp.sqrt(moment_two / (1.0 - BETA_TWO**STEP)) + ADAM_EPS)
    )
    return (weight - LR_VECTOR * direction, moment_one, moment_two)


def attend(query_row, key_row, segment_row):
    allowed = segment_row[:, None] == segment_row[None, :]
    logits = jnp.einsum("ihd,jhd->hij", query_row, key_row, preferred_element_type=jnp.float32)
    factor = 1.0 / math.sqrt(query_row.shape[-1])
    scores = jnp.where(allowed[None], logits * factor, -1e30)
    return (jax.nn.softmax(scores, axis=-1), allowed, factor)


def attend_forward(record):
    query_row, key_row, value_row, segment_row = record
    attn_probs, allowed, factor = attend(query_row, key_row, segment_row)
    return jnp.einsum(
        "hij,jhd->ihd",
        attn_probs.astype(jnp.bfloat16),
        value_row,
        preferred_element_type=jnp.float32,
    )


def attend_backward(record):
    query_row, key_row, value_row, segment_row, grad_row = record
    attn_probs, allowed, factor = attend(query_row, key_row, segment_row)
    probs_low = attn_probs.astype(jnp.bfloat16)
    grad_probs = jnp.einsum("ihd,jhd->hij", grad_row, value_row, preferred_element_type=jnp.float32)
    grad_value = jnp.einsum("hij,ihd->jhd", probs_low, grad_row, preferred_element_type=jnp.float32)
    grad_scores = attn_probs * (
        grad_probs - jnp.sum(attn_probs * grad_probs, axis=-1, keepdims=True)
    )
    grad_logits = jnp.where(allowed[None], grad_scores * factor, 0.0).astype(jnp.bfloat16)
    grad_query = jnp.einsum(
        "hij,jhd->ihd", grad_logits, key_row, preferred_element_type=jnp.float32
    )
    grad_key = jnp.einsum(
        "hij,ihd->jhd", grad_logits, query_row, preferred_element_type=jnp.float32
    )
    return (grad_query, grad_key, grad_value)


def per_device(
    inputs,
    cotangent,
    span_lengths,
    pad_lengths,
    pairing,
    owner_slot,
    master,
    first_moment,
    second_moment,
    left_basis,
    right_basis,
    vector_master,
    vector_first,
    vector_second,
):
    pair_count = lax.axis_size("pair")
    data_count = lax.axis_size("dp")
    grad_scale = 1.0 / (pair_count * data_count)
    block_side = master.shape[-1]
    gathered = lax.all_gather(master.astype(jnp.bfloat16), "dp", axis=0, tiled=True)
    w_query, w_key, w_value, w_output, w_inner, w_outer = assemble(
        jnp.take(gathered, owner_slot, axis=0)
    )
    (
        gain_one,
        shift_one,
        gain_two,
        shift_two,
        bias_query,
        bias_value,
        bias_output,
        bias_outer,
        bias_inner,
    ) = split_vector(vector_master)
    row_count = inputs.shape[1]
    seq_len = inputs.shape[2]
    token_count = row_count * seq_len
    heads_shape = (row_count, seq_len, HEADS, D // HEADS)
    flat_input = inputs.reshape(token_count, D)
    span_rows = span_lengths[0]
    pad_rows = pad_lengths[0]
    span_ends = jnp.cumsum(span_rows, axis=-1)
    span_starts = span_ends - span_rows
    positions = jnp.arange(seq_len, dtype=jnp.int32)
    inside = jnp.sum(
        (positions[None, :, None] >= span_ends[:, None, :-1]).astype(jnp.int32), axis=-1
    )
    segment_id = jnp.where(positions[None, :] >= seq_len - pad_rows[:, None], SEGS, inside)
    query_rows = (
        (jnp.dot(flat_input, w_query, preferred_element_type=jnp.float32) + bias_query)
        .astype(jnp.bfloat16)
        .reshape(heads_shape)
    )
    key_rows = (
        jnp.dot(flat_input, w_key, preferred_element_type=jnp.float32)
        .astype(jnp.bfloat16)
        .reshape(heads_shape)
    )
    value_rows = (
        (jnp.dot(flat_input, w_value, preferred_element_type=jnp.float32) + bias_value)
        .astype(jnp.bfloat16)
        .reshape(heads_shape)
    )
    mixed_heads = lax.map(attend_forward, (query_rows, key_rows, value_rows, segment_id))
    mixed_low = mixed_heads.reshape(token_count, D).astype(jnp.bfloat16)
    branch = jnp.dot(mixed_low, w_output, preferred_element_type=jnp.float32) + bias_output
    residual_one = flat_input.astype(jnp.float32) + branch
    normed = layer_norm(residual_one, gain_one, shift_one)
    normed_low = normed.astype(jnp.bfloat16)
    inner_sum = jnp.dot(normed_low, w_inner, preferred_element_type=jnp.float32) + bias_inner
    active_low = gelu_exact(inner_sum).astype(jnp.bfloat16)
    outer_sum = jnp.dot(active_low, w_outer, preferred_element_type=jnp.float32) + bias_outer
    residual_two = normed + outer_sum
    result = layer_norm(residual_two, gain_two, shift_two)
    result_rows = result.reshape(row_count, seq_len, D)
    leaders = jnp.take_along_axis(result_rows, span_starts[:, :, None], axis=1).reshape(-1, D)
    partner = swapped(leaders.astype(jnp.bfloat16), "pair", 0).astype(jnp.float32)
    pair_logits = (
        jnp.dot(leaders, partner.T, precision=HIGHEST, preferred_element_type=jnp.float32)
        * CLS_SCALE
    )
    pair_probs = jax.nn.softmax(pair_logits, axis=-1)
    targets = (
        pairing.reshape(-1)[:, None] == jnp.arange(leaders.shape[0], dtype=jnp.int32)[None, :]
    ).astype(jnp.float32)
    grad_pair = CLS_WEIGHT * CLS_SCALE * (pair_probs - targets)
    grad_leaders = jnp.dot(
        grad_pair, partner, precision=HIGHEST, preferred_element_type=jnp.float32
    )
    grad_partner = jnp.dot(
        grad_pair.T, leaders, precision=HIGHEST, preferred_element_type=jnp.float32
    )
    returned = swapped(grad_partner.astype(jnp.bfloat16), "pair", 0).astype(jnp.float32)
    grad_leaders = grad_leaders + returned
    valid_mask = (segment_id < SEGS).astype(jnp.float32)
    grad_result = cotangent[0].astype(jnp.float32) * valid_mask[:, :, None]
    row_index = jnp.arange(row_count, dtype=jnp.int32)[:, None]
    grad_result = grad_result.at[row_index, span_starts].add(
        grad_leaders.reshape(row_count, SEGS, D)
    )
    grad_result = grad_result.reshape(token_count, D)
    primal_two, norm_two_back = jax.vjp(layer_norm, residual_two, gain_two, shift_two)
    grad_residual_two, grad_gain_two, grad_shift_two = norm_two_back(grad_result)
    grad_outer = grad_residual_two.astype(jnp.bfloat16)
    grad_bias_outer = jnp.sum(grad_outer, axis=0, dtype=jnp.float32)
    grad_w_outer = jnp.einsum(
        "tf,td->fd", active_low, grad_outer, preferred_element_type=jnp.float32
    )
    grad_active = jnp.einsum("td,fd->tf", grad_outer, w_outer, preferred_element_type=jnp.float32)
    primal_gelu, gelu_back = jax.vjp(gelu_exact, inner_sum)
    grad_inner = gelu_back(grad_active)[0].astype(jnp.bfloat16)
    grad_bias_inner = jnp.sum(grad_inner, axis=0, dtype=jnp.float32)
    grad_w_inner = jnp.einsum(
        "td,tf->df", normed_low, grad_inner, preferred_element_type=jnp.float32
    )
    grad_normed = grad_residual_two + jnp.einsum(
        "tf,df->td", grad_inner, w_inner, preferred_element_type=jnp.float32
    )
    primal_one, norm_one_back = jax.vjp(layer_norm, residual_one, gain_one, shift_one)
    grad_residual_one, grad_gain_one, grad_shift_one = norm_one_back(grad_normed)
    grad_branch = grad_residual_one.astype(jnp.bfloat16)
    grad_bias_output = jnp.sum(grad_branch, axis=0, dtype=jnp.float32)
    grad_w_output = jnp.einsum(
        "td,te->de", mixed_low, grad_branch, preferred_element_type=jnp.float32
    )
    grad_mixed = (
        jnp.einsum("te,de->td", grad_branch, w_output, preferred_element_type=jnp.float32)
        .astype(jnp.bfloat16)
        .reshape(heads_shape)
    )
    grad_query, grad_key, grad_value = lax.map(
        attend_backward, (query_rows, key_rows, value_rows, segment_id, grad_mixed)
    )
    grad_query = grad_query.reshape(token_count, D).astype(jnp.bfloat16)
    grad_key = grad_key.reshape(token_count, D).astype(jnp.bfloat16)
    grad_value = grad_value.reshape(token_count, D).astype(jnp.bfloat16)
    grad_bias_query = jnp.sum(grad_query, axis=0, dtype=jnp.float32)
    grad_bias_value = jnp.sum(grad_value, axis=0, dtype=jnp.float32)
    grad_w_query = jnp.einsum(
        "td,te->de", flat_input, grad_query, preferred_element_type=jnp.float32
    )
    grad_w_key = jnp.einsum("td,te->de", flat_input, grad_key, preferred_element_type=jnp.float32)
    grad_w_value = jnp.einsum(
        "td,te->de", flat_input, grad_value, preferred_element_type=jnp.float32
    )
    grad_inputs = grad_residual_one + jnp.einsum(
        "te,de->td", grad_query, w_query, preferred_element_type=jnp.float32
    )
    grad_inputs = grad_inputs + jnp.einsum(
        "te,de->td", grad_key, w_key, preferred_element_type=jnp.float32
    )
    grad_inputs = grad_inputs + jnp.einsum(
        "te,de->td", grad_value, w_value, preferred_element_type=jnp.float32
    )
    local_vector = (
        jnp.concatenate(
            [
                grad_gain_one,
                grad_shift_one,
                grad_gain_two,
                grad_shift_two,
                grad_bias_query,
                grad_bias_value,
                grad_bias_output,
                grad_bias_outer,
                grad_bias_inner,
            ]
        )
        * grad_scale
    )
    vector_grad = lax.psum(local_vector, ("pair", "dp"))
    grad_blocks = (
        disassemble(
            (grad_w_query, grad_w_key, grad_w_value, grad_w_output, grad_w_inner, grad_w_outer),
            block_side,
        )
        * grad_scale
    )
    slot_total = master.shape[0] * data_count
    dealt_grad = (
        jnp.zeros((slot_total, block_side, block_side), jnp.float32).at[owner_slot].set(grad_blocks)
    )
    owned_grad = lax.psum_scatter(dealt_grad, "dp", scatter_dimension=0, tiled=True)
    owned_grad = lax.psum(owned_grad.astype(jnp.bfloat16), "pair").astype(jnp.float32)
    new_master, new_first, new_second = soap_update(
        owned_grad, master, first_moment, second_moment, left_basis, right_basis
    )
    new_vector, vector_one, vector_two = adam_update(
        vector_grad, vector_master, vector_first, vector_second
    )
    return (
        result_rows.astype(jnp.bfloat16).reshape(inputs.shape),
        grad_inputs.reshape(inputs.shape),
        owned_grad,
        new_master,
        new_first,
        new_second,
        vector_grad,
        jnp.stack([new_vector, vector_one, vector_two], axis=0),
    )


def solution(mesh):
    placed = (
        P("pair", "dp", None, None),
        P("pair", "dp", None, None),
        P("pair", "dp", None),
        P("pair", "dp"),
        P("pair", "dp", None),
        P(),
        P("dp", None, None),
        P("dp", None, None),
        P("dp", None, None),
        P("dp", None, None),
        P("dp", None, None),
        P(),
        P(),
        P(),
    )
    return jax.shard_map(
        per_device,
        mesh=mesh,
        in_specs=placed,
        out_specs=(
            P("pair", "dp", None, None),
            P("pair", "dp", None, None),
            P("dp", None, None),
            P("dp", None, None),
            P("dp", None, None),
            P("dp", None, None),
            P(),
            P(),
        ),
        check_vma=False,
    )
```

profile of v0, /device:TPU:0, one launch (start us, length us, event | category | flops | bytes accessed | tf_op | source)
XLA Modules:
  0.0 1472.3 jit_solution(17176279958069419117)
XLA Ops:
  14.8 170.6 %all-gather.2.cloned.1.call-done = bf16[112,256,256]{2,1,0:T(8,128)(2,1)} async-done(((bf16[7,256,256]{2,1,0:T(8,128)(2,1)}), bf16[112,256,256]{2,1,0:T(8,128)(2,1)}) %all-gather.2.cloned.1.call-update) | async-done | bytes 14680080 | tf_op jit(solution)/shard_map/all_gather | solution.py:174
  185.4 12.7 gather_fusion
  254.2 36.5 %while.24 = (s32[]{:T(128)}, bf16[2,512,12,64]{1,3,2,0:T(8,128)(2,1)}, bf16[2,512,12,64]{1,3,2,0:T(8,128)(2,1)S(1)}, s32[2,512]{1,0:T(2,128)S(1)}, bf16[2,512,12...) while((s32[]{:T(128)}, bf16[2,512,12,64]{1,3,2,0:T(8,128)(2,1)}, ...), condition=%wide.region_5.6_spmd, body=%wide.region_2.5_spmd.sunk | while | flops 824443392 | bytes 29687888 | solution.py:218
  255.1 10.5 fusion.244
  324.2 34.9 %multiply_convert_fusion = (bf16[1024,3072]{1,0:T(8,128)(2,1)S(1)}, f32[1024,3072]{1,0:T(8,128)}, f32[1024,3072]{1,0:T(8,128)}) fusion(f32[3072]{0:T(1024)S(1)} %copy-done.65, bf16[768,3072]{1,0:T(8,128)(2,1)S(1)} %bitcast.340, f32[1024,768]{1,0:T(8,128)S(1)} %copy-done.6, f32[768]{0:T(1024)S(1)} %copy-done.50, f32[768]{0:T(1024)S(1)} %copy-done.49, ...), kind=kOutput, calls=%fused_computation.93 | convolution fusion | flops 5043388416 | bytes 39348224 | tf_op jit(solution)/shard_map/dot_general | solution.py:224
  383.2 17.4 %convert_reduce_fusion = (f32[3072]{0:T(1024)}, bf16[1024,3072]{1,0:T(8,128)(2,1)}) fusion(f32[1024,3072]{1,0:T(8,128)} %get-tuple-element.243, bf16[1024,768]{1,0:T(8,128)(2,1)S(1)} %get-tuple-element.231, bf16[3072,768]{0,1:T(8,128)(2,1)} %bitcast.342, f32[1024,3072]{1,0:T(8,128)} %get-tuple-element.268, f32[3072]{0:T(1024)S(1)} %copy-done.65), kind=kOutput, calls=%fused_computation.91 | convolution fusion | flops 4885312512 | bytes 37773312 | tf_op jit(solution)/shard_map/td,fd->tf/dot_general | solution.py:263
  448.8 128.8 %while.25 = (s32[]{:T(128)}, bf16[2,512,12,64]{1,3,2,0:T(8,128)(2,1)}, bf16[2,512,12,64]{1,3,2,0:T(8,128)(2,1)}, bf16[2,512,12,64]{1,3,2,0:T(8,128)(2,1)}, bf16[...) while((s32[]{:T(128)}, ...), condition=%wide.region_21.22_spmd, body=%wide.region_17.21_spmd.sunk | while | flops 2082747904 | bytes 149875824 | solution.py:285
  450.1 10.6 fusion.256
  468.2 18.7 %bitcast_dynamic-update-slice_fusion.10 = bf16[2,512,12,64]{1,3,2,0:T(8,128)(2,1)} fusion(bf16[2,512,12,64]{1,3,2,0:T(8,128)(2,1)} %get-tuple-element.411, s32[]{:T(128)} %get-tuple-element.409, f32[12,512,512]{1,2,0:T(8,128)} %fusion.255, pred[512,512]{0,1:T(8,128)(4,1)} %broadcast_compare_fusion.5, ...), kind=kOutput, calls=%fused_computation.50.clone.1 | convolution fusion | flops 427825664 | bytes 53019648 | tf_op jit(solution)/shard_map/while/body/eval_jaxpr/hij,ihd->jhd/dot_general | solution.py:148
  494.7 18.7 %bitcast_dynamic-update-slice_fusion.9 = bf16[2,512,12,64]{1,3,2,0:T(8,128)(2,1)} fusion(bf16[2,512,12,64]{1,3,2,0:T(8,128)(2,1)} %get-tuple-element.410, s32[]{:T(128)} %get-tuple-element.409, f32[12,512,512]{1,2,0:T(8,128)} %fusion.255, pred[512,512]{0,1:T(8,128)(4,1)} %broadcast_compare_fusion.5, ...), kind=kOutput, calls=%fused_computation.51.clone.1 | convolution fusion | flops 427825664 | bytes 53019648 | tf_op jit(solution)/shard_map/while/body/eval_jaxpr/hij,jhd->ihd/dot_general | solution.py:145
  514.3 10.6 fusion.256
  532.3 18.8 %bitcast_dynamic-update-slice_fusion.10 = bf16[2,512,12,64]{1,3,2,0:T(8,128)(2,1)} fusion(bf16[2,512,12,64]{1,3,2,0:T(8,128)(2,1)} %get-tuple-element.411, s32[]{:T(128)} %get-tuple-element.409, f32[12,512,512]{1,2,0:T(8,128)} %fusion.255, pred[512,512]{0,1:T(8,128)(4,1)} %broadcast_compare_fusion.5, ...), kind=kOutput, calls=%fused_computation.50.clone.1 | convolution fusion | flops 427825664 | bytes 53019648 | tf_op jit(solution)/shard_map/while/body/eval_jaxpr/hij,ihd->jhd/dot_general | solution.py:148
  558.9 18.7 %bitcast_dynamic-update-slice_fusion.9 = bf16[2,512,12,64]{1,3,2,0:T(8,128)(2,1)} fusion(bf16[2,512,12,64]{1,3,2,0:T(8,128)(2,1)} %get-tuple-element.410, s32[]{:T(128)} %get-tuple-element.409, f32[12,512,512]{1,2,0:T(8,128)} %fusion.255, pred[512,512]{0,1:T(8,128)(4,1)} %broadcast_compare_fusion.5, ...), kind=kOutput, calls=%fused_computation.51.clone.1 | convolution fusion | flops 427825664 | bytes 53019648 | tf_op jit(solution)/shard_map/while/body/eval_jaxpr/hij,jhd->ihd/dot_general | solution.py:145
  577.6 12.2 reshape.392
  589.8 13.8 copy.170
  659.0 12.0 reshape.394
  670.9 12.4 copy.172
  707.0 20.0 %broadcast_multiply_fusion = f32[108,256,256]{2,1,0:T(8,128)} fusion(f32[108,256,256]{2,1,0:T(8,128)} %constant_dynamic-update-slice_fusion), kind=kLoop, calls=%fused_computation.88 | loop fusion | flops 7077888 | bytes 56623104 | tf_op jit(solution)/shard_map/mul | solution.py:327
  727.0 13.4 broadcast_in_dim.136
  740.3 51.8 %scatter_fusion.1 = f32[112,256,256]{2,1,0:T(8,128)} fusion(f32[112,256,256]{2,1,0:T(8,128)} %broadcast_in_dim.136, s32[108]{0:T(128)S(1)} %copy-done.71, f32[108,256,256]{2,1,0:T(8,128)} %broadcast_multiply_fusion), kind=kCustom, calls=%fused_computation.3 | custom fusion | bytes 84935088 | tf_op jit(solution)/shard_map/scatter | solution.py:335
  792.2 29.6 %copy.173 = f32[112,256,256]{1,2,0:T(8,128)} copy(f32[112,256,256]{2,1,0:T(8,128)} %scatter_fusion.1) | data formatting | bytes 58720256 | tf_op jit(solution)/shard_map/scatter | solution.py:335
  826.2 78.5 %psum.15 = f32[9216]{0:T(1024)S(1)} all-reduce(f32[9216]{0:T(1024)S(1)} %broadcast_multiply_fusion.1), channel_id=1, replica_groups=mesh['pair'=2,'dp'=16] {'pair','dp'}, use_global_device_ids=true, to_apply=%region_34.35 | all-reduce | flops 9216 | bytes 73728 | tf_op jit(solution)/shard_map/psum | solution.py:325
  914.5 508.5 %reduce-scatter.2.cloned.1.call-done = f32[7,256,256]{1,2,0:T(8,128)} async-done(((f32[112,256,256]{1,2,0:T(8,128)}), f32[7,256,256]{1,2,0:T(8,128)}) %reduce-scatter.2.cloned.1.call-update) | async-done | bytes 1835024 | tf_op jit(solution)/shard_map/reduce_scatter | solution.py:337
  1426.3 25.0 %all-reduce.2.cloned.1.call-done = bf16[7,256,256]{1,2,0:T(8,128)(2,1)} async-done(((bf16[7,256,256]{1,2,0:T(8,128)(2,1)}), bf16[7,256,256]{1,2,0:T(8,128)(2,1)}) %all-reduce.2.cloned.1.call-update) | async-done | bytes 917520 | tf_op jit(solution)/shard_map/psum | solution.py:338
  (344 shorter events, 337.0 us)
Async XLA Ops:
  7.2 1447.7 %copy-start = (f32[7,256,256]{2,1,0:T(8,128)S(1)}, f32[7,256,256]{2,1,0:T(8,128)}, u32[]{:S(2)}) copy-start(f32[7,256,256]{2,1,0:T(8,128)} %param.28) | copy-start | bytes 5505028
  7.2 5.7 copy-start.83
  7.2 178.1 %all-gather.2.cloned.1.call-start = ((), (), s32[]{:S(2)}) async-start(), calls=%async_computation.1 | async-start | bytes 15597568 | tf_op jit(solution)/shard_map/all_gather | solution.py:174
  9.9 1413.1 %reduce-scatter.2.cloned.1.call-start = ((), (), s32[]{:S(2)}) async-start(), calls=%async_computation.2 | async-start | bytes 31195136 | tf_op jit(solution)/shard_map/reduce_scatter | solution.py:337
  309.2 14.9 %slice-start.5 = ((s8[4718592]{0:T(1024)(128)(4,1)}), s8[524288]{0:T(1024)(128)(4,1)S(1)}, s32[]{:S(2)}) async-start(s8[4718592]{0:T(1024)(128)(4,1)} %bitcast.338), calls=%async_computation.9 | async-start | bytes 1048576
  317.9 6.2 copy-start.6
  317.9 6.2 slice-start.6
  317.9 6.2 copy-start.49
  317.9 6.2 copy-start.50
  318.0 6.2 copy-start.65
  324.1 35.0 %copy-start.26 = (bf16[96,8,12,256]{3,1,2,0:T(8,128)(2,1)}, bf16[96,8,12,256]{3,1,2,0:T(8,128)(2,1)S(1)}, u32[]{:S(2)}) copy-start(bf16[96,8,12,256]{3,1,2,0:T(8,128)(2,1)S(1)} %copy.193) | copy-start | bytes 14155780
  324.2 35.0 %copy-start.66 = (f32[768]{0:T(1024)S(1)}, f32[768]{0:T(1024)}, u32[]{:S(2)}) copy-start(f32[768]{0:T(1024)} %get-tuple-element.256) | copy-start | bytes 9220
  365.3 6.1 copy-start.38
  365.3 6.1 copy-start.62
  369.5 1.2 collective-permute-start
  371.1 2.4 collective-permute-start.1
  383.2 17.4 %copy-start.7 = (f32[1024,768]{1,0:T(8,128)S(1)}, f32[1024,768]{1,0:T(8,128)}, u32[]{:S(2)}) copy-start(f32[1024,768]{1,0:T(8,128)} %copy-done.5) | copy-start | bytes 9437188
  400.6 10.5 copy-start.15
  419.7 10.3 copy-start.55
  589.8 13.8 copy-start.12
  683.4 10.6 slice-start
  686.8 7.2 slice-start.1
  727.0 13.4 copy-start.71
  821.8 629.5 %all-reduce.2.cloned.1.call-start = ((), (), s32[]{:S(2)}) async-start(), calls=%async_computation.3 | async-start | bytes 1835008 | tf_op jit(solution)/shard_map/psum | solution.py:338
  (73 other events, 223.3 us)
Sparse Core Ops, SparseCore 0:
  11.4 173.9 all-gather.1
  821.9 601.0 reduce-scatter.1
  1425.9 25.3 all-reduce.1
where the time goes:
time: 1480 us; the launch traced here: 1470 us
  waiting for transfers between devices  705 us (48%)
  local copies, waits for them, and re-layouts  319 us (22%)
  matrix products  292 us (20%)
  blocking collectives  78.5 us (5%)
  other arithmetic  61.1 us (4%)
  between operations  15.3 us (1%)
    reduce_scatter x1, waiting for transfers between devices, per_device(): lax.psum_scatter(dealt_grad, 'dp', scatter_dimension=0, tiled=True)  509 us
    all_gather x1, waiting for transfers between devices, per_device(): lax.all_gather(master.astype(jnp.bfloat16), 'dp', axis=0, tiled=True)  171 us
    scatter x2, local copies, waits for them, and re-layouts, per_device(): jnp.zeros((slot_total, block_side, block_side), jnp.float32).at[owner_slot]  81.4 us
    psum x1, blocking collectives, per_device(): vector_grad = lax.psum(local_vector, ('pair', 'dp'))  78.5 us
    unnamed x208, local copies, waits for them, and re-layouts  48.8 us
    sub x4, matrix products, attend(): return (jax.nn.softmax(scores, axis=-1), allowed, factor)  42.2 us
    reshape x5, local copies, waits for them, and re-layouts, untiled(): matrix.reshape(count_rows, block_side, count_cols, block_side)  38 us
    dot_general x2, matrix products, attend_backward(): jnp.einsum('hij,ihd->jhd', grad_logits, query_row, preferred_element_type...  37.5 us
  transfers between devices with their start and end apart: 5, of which 4 were waited for; matrix products, arithmetic and copies ran while one was open for 1% of the time, Pallas kernels for 0%

commit v1 on v0

--- a/solution.py
+++ b/solution.py
@@ -171,7 +171,25 @@
     data_count = lax.axis_size("dp")
     grad_scale = 1.0 / (pair_count * data_count)
     block_side = master.shape[-1]
-    gathered = lax.all_gather(master.astype(jnp.bfloat16), "dp", axis=0, tiled=True)
+    x = master.astype(jnp.bfloat16)
+    size, position, rows = (lax.axis_size("dp"), lax.axis_index("dp"), x.shape[0])
+    forward = [(i_2, (i_2 + 1) % size) for i_2 in range(size)]
+    left = [(i_2, (i_2 - 1) % size) for i_2 in range(size)]
+    out = jnp.zeros((*x.shape[:0], size * rows, *x.shape[0 + 1 :]), x.dtype)
+    out = lax.dynamic_update_slice_in_dim(out, x, position * rows, axis=0)
+    from_left = from_right = x
+    half = size // 2
+    for lap in range(1, half + 1):
+        from_left = lax.ppermute(from_left, "dp", forward)
+        out = lax.dynamic_update_slice_in_dim(
+            out, from_left, (position - lap) % size * rows, axis=0
+        )
+        if lap < size - half:
+            from_right = lax.ppermute(from_right, "dp", left)
+            out = lax.dynamic_update_slice_in_dim(
+                out, from_right, (position + lap) % size * rows, axis=0
+            )
+    gathered = out
     w_query, w_key, w_value, w_output, w_inner, w_outer = assemble(
         jnp.take(gathered, owner_slot, axis=0)
     )

time: 1480 us -> 1620 us (1.095)
  starting transfers between devices: 0.36 us -> 90.2 us
  local copies, waits for them, and re-layouts: 319 us -> 346 us
    ppermute x0 -> x15, waiting for transfers between devices: none -> 184 us  [the longest x8 172 us: per_device(): from_left = lax.ppermute(from_left, 'dp', forward)]
    all_gather x1 -> x0, waiting for transfers between devices: 171 us -> none  [per_device(): lax.all_gather(master.astype(jnp.bfloat16), 'dp', axis=0, tiled=True)]
    ppermute x0 -> x15, starting transfers between devices: none -> 89.8 us  [the longest x7 74.2 us: per_device(): from_right = lax.ppermute(from_right, 'dp', left)]
    dynamic_update_slice x0 -> x15, local copies, waits for them, and re-layouts: none -> 23.4 us  [the longest x7 11.8 us: per_device(): lax.dynamic_update_slice_in_dim(out, from_right, (position + lap) % size...]
    unnamed x208 -> x230, local copies, waits for them, and re-layouts: 48.8 us -> 50.5 us
  transfers between devices with their start and end apart: 5 -> 19, of which waited for: 4 -> 11; matrix products, arithmetic and copies ran while one was open for 1% -> 3% of each run, Pallas kernels for 0% -> 0%
where the time goes in v1:
time: 1620 us; the launch traced here: 1610 us
  waiting for transfers between devices  719 us (44%)
  local copies, waits for them, and re-layouts  346 us (21%)
  matrix products  288 us (18%)
  blocking collectives  92.1 us (6%)
  starting transfers between devices  90.2 us (6%)
  other arithmetic  61.2 us (4%)
    reduce_scatter x1, waiting for transfers between devices, per_device(): lax.psum_scatter(dealt_grad, 'dp', scatter_dimension=0, tiled=True)  509 us
    ppermute x8, waiting for transfers between devices, per_device(): from_left = lax.ppermute(from_left, 'dp', forward)  172 us
    psum x1, blocking collectives, per_device(): vector_grad = lax.psum(local_vector, ('pair', 'dp'))  92.1 us
    scatter x2, local copies, waits for them, and re-layouts, per_device(): jnp.zeros((slot_total, block_side, block_side), jnp.float32).at[owner_slot]  81.5 us
    ppermute x7, starting transfers between devices, per_device(): from_right = lax.ppermute(from_right, 'dp', left)  74.2 us
    unnamed x230, local copies, waits for them, and re-layouts  50.5 us
    sub x4, matrix products, attend(): return (jax.nn.softmax(scores, axis=-1), allowed, factor)  42.4 us
    reshape x5, local copies, waits for them, and re-layouts, untiled(): matrix.reshape(count_rows, block_side, count_cols, block_side)  38.4 us
  transfers between devices with their start and end apart: 19, of which 11 were waited for; matrix products, arithmetic and copies ran while one was open for 3% of the time, Pallas kernels for 0%

profile of v1, /device:TPU:0, one launch (start us, length us, event | category | flops | bytes accessed | tf_op | source)
XLA Modules:
  0.0 1613.5 jit_solution(6170324500959254037)
XLA Ops:
  23.9 35.3 %collective-permute-done = bf16[7,256,256]{2,1,0:T(8,128)(2,1)S(1)} collective-permute-done((bf16[7,256,256]{2,1,0:T(8,128)(2,1)S(1)}, bf16[7,256,256]{2,1,0:T(8,128)(2,1)S(1)}, u32[]{:S(2)}, u32[]{:S(2)}) %collective-permute-start) | collective-permute-done | bytes 917536 | tf_op jit(solution)/shard_map/ppermute | solution.py:183
  64.8 35.3 %collective-permute-done.2 = bf16[7,256,256]{2,1,0:T(8,128)(2,1)S(1)} collective-permute-done((bf16[7,256,256]{2,1,0:T(8,128)(2,1)S(1)}, bf16[7,256,256]{2,1,0:T(8,128)(2,1)S(1)}, u32[]{:S(2)}, u32[]{:S(2)}) %collective-permute-start.2) | collective-permute-done | bytes 917536 | tf_op jit(solution)/shard_map/ppermute | solution.py:183
  105.7 34.4 %collective-permute-done.4 = bf16[7,256,256]{2,1,0:T(8,128)(2,1)S(1)} collective-permute-done((bf16[7,256,256]{2,1,0:T(8,128)(2,1)S(1)}, bf16[7,256,256]{2,1,0:T(8,128)(2,1)S(1)}, u32[]{:S(2)}, u32[]{:S(2)}) %collective-permute-start.4) | collective-permute-done | bytes 917536 | tf_op jit(solution)/shard_map/ppermute | solution.py:183
  145.7 34.3 %collective-permute-done.6 = bf16[7,256,256]{2,1,0:T(8,128)(2,1)} collective-permute-done((bf16[7,256,256]{2,1,0:T(8,128)(2,1)S(1)}, bf16[7,256,256]{2,1,0:T(8,128)(2,1)}, u32[]{:S(2)}, u32[]{:S(2)}) %collective-permute-start.6) | collective-permute-done | bytes 917536 | tf_op jit(solution)/shard_map/ppermute | solution.py:183
  183.4 20.8 %collective-permute-start.9 = (bf16[7,256,256]{2,1,0:T(8,128)(2,1)}, bf16[7,256,256]{2,1,0:T(8,128)(2,1)}, u32[]{:S(2)}, u32[]{:S(2)}) collective-permute-start(bf16[7,256,256]{2,1,0:T(8,128)(2,1)} %collective-permute-done.7), channel_id=1, source_target_pairs={{0,15},{1,0},{2,1},{3,2},{4,3},{5,4},{6,5},{7,6},{8,7},{9,8},{10,9... | collective-permute-start | bytes 2752520 | tf_op jit(solution)/shard_map/ppermute | solution.py:188
  204.2 16.1 collective-permute-done.8
  226.2 18.9 %collective-permute-start.11 = (bf16[7,256,256]{2,1,0:T(8,128)(2,1)}, bf16[7,256,256]{2,1,0:T(8,128)(2,1)S(1)}, u32[]{:S(2)}, u32[]{:S(2)}) collective-permute-start(bf16[7,256,256]{2,1,0:T(8,128)(2,1)} %collective-permute-done.9), channel_id=1, source_target_pairs={{0,15},{1,0},{2,1},{3,2},{4,3},{5,4},{6,5},{7,6},{8,7},{9,8},{10,9... | collective-permute-start | bytes 2752520 | tf_op jit(solution)/shard_map/ppermute | solution.py:188
  263.9 21.0 %collective-permute-start.13 = (bf16[7,256,256]{2,1,0:T(8,128)(2,1)S(1)}, bf16[7,256,256]{2,1,0:T(8,128)(2,1)S(1)}, u32[]{:S(2)}, u32[]{:S(2)}) collective-permute-start(bf16[7,256,256]{2,1,0:T(8,128)(2,1)S(1)} %collective-permute-done.11), channel_id=1, source_target_pairs={{0,15},{1,0},{2,1},{3,2},{4,3},{5,4},{6,5},{7,6},{8,7},{9,8},{10,9... | collective-permute-start | bytes 2752520 | tf_op jit(solution)/shard_map/ppermute | solution.py:188
  301.5 16.4 %collective-permute-done.14 = bf16[7,256,256]{2,1,0:T(8,128)(2,1)S(1)} collective-permute-done((bf16[7,256,256]{2,1,0:T(8,128)(2,1)S(1)}, bf16[7,256,256]{2,1,0:T(8,128)(2,1)S(1)}, u32[]{:S(2)}, u32[]{:S(2)}) %collective-permute-start.14) | collective-permute-done | bytes 917536 | tf_op jit(solution)/shard_map/ppermute | solution.py:183
  387.6 36.8 %while.24 = (s32[]{:T(128)}, bf16[2,512,12,64]{1,3,2,0:T(8,128)(2,1)}, bf16[2,512,12,64]{1,3,2,0:T(8,128)(2,1)S(1)}, s32[2,512]{1,0:T(2,128)S(1)}, bf16[2,512,12...) while((s32[]{:T(128)}, bf16[2,512,12,64]{1,3,2,0:T(8,128)(2,1)}, ...), condition=%wide.region_5.6_spmd, body=%wide.region_2.5_spmd.sunk | while | flops 824443392 | bytes 29687888 | solution.py:236
  457.6 35.0 %multiply_convert_fusion = (bf16[1024,3072]{1,0:T(8,128)(2,1)S(1)}, f32[1024,3072]{1,0:T(8,128)}, f32[1024,3072]{1,0:T(8,128)}) fusion(f32[3072]{0:T(1024)S(1)} %copy-done.73, bf16[768,3072]{1,0:T(8,128)(2,1)S(1)} %bitcast.346, f32[1024,768]{1,0:T(8,128)S(1)} %copy-done.6, f32[768]{0:T(1024)S(1)} %copy-done.59, f32[768]{0:T(1024)S(1)} %copy-done.58, ...), kind=kOutput, calls=%fused_computation.93 | convolution fusion | flops 5043388416 | bytes 39348224 | tf_op jit(solution)/shard_map/dot_general | solution.py:242
  524.4 17.9 %convert_reduce_fusion = (f32[3072]{0:T(1024)}, bf16[1024,3072]{1,0:T(8,128)(2,1)}) fusion(f32[1024,3072]{1,0:T(8,128)} %get-tuple-element.220, bf16[1024,768]{1,0:T(8,128)(2,1)S(1)} %get-tuple-element.208, bf16[3072,768]{0,1:T(8,128)(2,1)} %bitcast.348, f32[1024,3072]{1,0:T(8,128)} %get-tuple-element.247, f32[3072]{0:T(1024)S(1)} %copy-done.73), kind=kOutput, calls=%fused_computation.91 | convolution fusion | flops 4885312512 | bytes 37773312 | tf_op jit(solution)/shard_map/td,fd->tf/dot_general | solution.py:281
  579.9 129.3 %while.25 = (s32[]{:T(128)}, bf16[2,512,12,64]{1,3,2,0:T(8,128)(2,1)}, bf16[2,512,12,64]{1,3,2,0:T(8,128)(2,1)}, bf16[2,512,12,64]{1,3,2,0:T(8,128)(2,1)}, bf16[...) while((s32[]{:T(128)}, ...), condition=%wide.region_21.22_spmd, body=%wide.region_17.21_spmd.sunk | while | flops 2082747904 | bytes 149875824 | solution.py:303
  599.1 19.0 %bitcast_dynamic-update-slice_fusion.10 = bf16[2,512,12,64]{1,3,2,0:T(8,128)(2,1)} fusion(bf16[2,512,12,64]{1,3,2,0:T(8,128)(2,1)} %get-tuple-element.390, s32[]{:T(128)} %get-tuple-element.388, f32[12,512,512]{1,2,0:T(8,128)} %fusion.255, pred[512,512]{0,1:T(8,128)(4,1)} %broadcast_compare_fusion.5, ...), kind=kOutput, calls=%fused_computation.50.clone.1 | convolution fusion | flops 427825664 | bytes 53019648 | tf_op jit(solution)/shard_map/while/body/eval_jaxpr/hij,ihd->jhd/dot_general | solution.py:148
  625.8 18.7 %bitcast_dynamic-update-slice_fusion.9 = bf16[2,512,12,64]{1,3,2,0:T(8,128)(2,1)} fusion(bf16[2,512,12,64]{1,3,2,0:T(8,128)(2,1)} %get-tuple-element.389, s32[]{:T(128)} %get-tuple-element.388, f32[12,512,512]{1,2,0:T(8,128)} %fusion.255, pred[512,512]{0,1:T(8,128)(4,1)} %broadcast_compare_fusion.5, ...), kind=kOutput, calls=%fused_computation.51.clone.1 | convolution fusion | flops 427825664 | bytes 53019648 | tf_op jit(solution)/shard_map/while/body/eval_jaxpr/hij,jhd->ihd/dot_general | solution.py:145
  663.6 19.0 %bitcast_dynamic-update-slice_fusion.10 = bf16[2,512,12,64]{1,3,2,0:T(8,128)(2,1)} fusion(bf16[2,512,12,64]{1,3,2,0:T(8,128)(2,1)} %get-tuple-element.390, s32[]{:T(128)} %get-tuple-element.388, f32[12,512,512]{1,2,0:T(8,128)} %fusion.255, pred[512,512]{0,1:T(8,128)(4,1)} %broadcast_compare_fusion.5, ...), kind=kOutput, calls=%fused_computation.50.clone.1 | convolution fusion | flops 427825664 | bytes 53019648 | tf_op jit(solution)/shard_map/while/body/eval_jaxpr/hij,ihd->jhd/dot_general | solution.py:148
  690.4 18.8 %bitcast_dynamic-update-slice_fusion.9 = bf16[2,512,12,64]{1,3,2,0:T(8,128)(2,1)} fusion(bf16[2,512,12,64]{1,3,2,0:T(8,128)(2,1)} %get-tuple-element.389, s32[]{:T(128)} %get-tuple-element.388, f32[12,512,512]{1,2,0:T(8,128)} %fusion.255, pred[512,512]{0,1:T(8,128)(4,1)} %broadcast_compare_fusion.5, ...), kind=kOutput, calls=%fused_computation.51.clone.1 | convolution fusion | flops 427825664 | bytes 53019648 | tf_op jit(solution)/shard_map/while/body/eval_jaxpr/hij,jhd->ihd/dot_general | solution.py:145
  745.7 13.7 copy.127
  834.2 20.0 %broadcast_multiply_fusion = f32[108,256,256]{2,1,0:T(8,128)} fusion(f32[108,256,256]{2,1,0:T(8,128)} %constant_dynamic-update-slice_fusion), kind=kLoop, calls=%fused_computation.88 | loop fusion | flops 7077888 | bytes 56623104 | tf_op jit(solution)/shard_map/mul | solution.py:345
  867.5 52.0 %scatter_fusion.1 = f32[112,256,256]{2,1,0:T(8,128)} fusion(f32[112,256,256]{2,1,0:T(8,128)} %broadcast_in_dim.140, s32[108]{0:T(128)S(1)} %copy-done.80, f32[108,256,256]{2,1,0:T(8,128)} %broadcast_multiply_fusion), kind=kCustom, calls=%fused_computation.3 | custom fusion | bytes 84935088 | tf_op jit(solution)/shard_map/scatter | solution.py:353
  919.5 29.6 %copy.130 = f32[112,256,256]{1,2,0:T(8,128)} copy(f32[112,256,256]{2,1,0:T(8,128)} %scatter_fusion.1) | data formatting | bytes 58720256 | tf_op jit(solution)/shard_map/scatter | solution.py:353
  953.7 92.1 %psum.15 = f32[9216]{0:T(1024)S(1)} all-reduce(f32[9216]{0:T(1024)S(1)} %broadcast_multiply_fusion.1), channel_id=1, replica_groups=mesh['pair'=2,'dp'=16] {'pair','dp'}, use_global_device_ids=true, to_apply=%region_34.35 | all-reduce | flops 9216 | bytes 73728 | tf_op jit(solution)/shard_map/psum | solution.py:343
  1055.1 509.3 %reduce-scatter.2.cloned.1.call-done = f32[7,256,256]{1,2,0:T(8,128)} async-done(((f32[112,256,256]{1,2,0:T(8,128)}), f32[7,256,256]{1,2,0:T(8,128)}) %reduce-scatter.2.cloned.1.call-update) | async-done | bytes 1835024 | tf_op jit(solution)/shard_map/reduce_scatter | solution.py:355
  1567.7 24.5 %all-reduce.2.cloned.1.call-done = bf16[7,256,256]{1,2,0:T(8,128)(2,1)} async-done(((bf16[7,256,256]{1,2,0:T(8,128)(2,1)}), bf16[7,256,256]{1,2,0:T(8,128)(2,1)}) %all-reduce.2.cloned.1.call-update) | async-done | bytes 917520 | tf_op jit(solution)/shard_map/psum | solution.py:356
  (410 shorter events, 495.4 us)
Async XLA Ops:
  7.2 1588.6 %copy-start = (f32[7,256,256]{2,1,0:T(8,128)S(1)}, f32[7,256,256]{2,1,0:T(8,128)}, u32[]{:S(2)}) copy-start(f32[7,256,256]{2,1,0:T(8,128)} %param.28) | copy-start | bytes 5505028
  7.2 1557.2 %reduce-scatter.2.cloned.1.call-start = ((), (), s32[]{:S(2)}) async-start(), calls=%async_computation.1 | async-start | bytes 31195136 | tf_op jit(solution)/shard_map/reduce_scatter | solution.py:355
  14.3 168.4 %copy-start.78 = (s32[1,2,4]{2,1,0:T(2,128)S(1)}, s32[1,2,4]{2,1,0:T(2,128)}, u32[]{:S(2)}) copy-start(s32[1,2,4]{2,1,0:T(2,128)} %param.20) | copy-start | bytes 100
  14.3 168.5 %copy-start.91 = (s32[108]{0:T(128)S(1)}, s32[108]{0:T(128)}, u32[]{:S(2)}) copy-start(s32[108]{0:T(128)} %param.23) | copy-start | bytes 1300
  14.3 208.5 %copy-start.92 = (s32[1,2]{1,0:T(1,128)S(1)}, s32[1,2]{1,0:T(1,128)}, u32[]{:S(2)}) copy-start(s32[1,2]{1,0:T(1,128)} %param.21) | copy-start | bytes 28
  14.3 208.8 %copy-start.53 = (f32[9216]{0:T(1024)S(1)}, f32[9216]{0:T(1024)}, u32[]{:S(2)}) copy-start(f32[9216]{0:T(1024)} %param.29) | copy-start | bytes 110596
  16.9 42.2 %collective-permute-start = (bf16[7,256,256]{2,1,0:T(8,128)(2,1)S(1)}, bf16[7,256,256]{2,1,0:T(8,128)(2,1)S(1)}, u32[]{:S(2)}, u32[]{:S(2)}) collective-permute-start(bf16[7,256,256]{2,1,0:T(8,128)(2,1)S(1)} %get-tuple-element.222), channel_id=1, source_target_pairs={{0,1},{1,2},{2,3},{3,4},{4,5},{5,6},{6,7},{7,8},{8,9},{9,10},{10,1... | collective-permute-start | bytes 2752520 | tf_op jit(solution)/shard_map/ppermute | solution.py:183
  19.9 41.8 %collective-permute-start.1 = (bf16[7,256,256]{2,1,0:T(8,128)(2,1)S(1)}, bf16[7,256,256]{2,1,0:T(8,128)(2,1)S(1)}, u32[]{:S(2)}, u32[]{:S(2)}) collective-permute-start(bf16[7,256,256]{2,1,0:T(8,128)(2,1)S(1)} %get-tuple-element.222), channel_id=1, source_target_pairs={{0,15},{1,0},{2,1},{3,2},{4,3},{5,4},{6,5},{7,6},{8,7},{9,8},{10,9... | collective-permute-start | bytes 2752520 | tf_op jit(solution)/shard_map/ppermute | solution.py:188
  59.1 40.9 %collective-permute-start.2 = (bf16[7,256,256]{2,1,0:T(8,128)(2,1)S(1)}, bf16[7,256,256]{2,1,0:T(8,128)(2,1)S(1)}, u32[]{:S(2)}, u32[]{:S(2)}) collective-permute-start(bf16[7,256,256]{2,1,0:T(8,128)(2,1)S(1)} %collective-permute-done), channel_id=1, source_target_pairs={{0,1},{1,2},{2,3},{3,4},{4,5},{5,6},{6,7},{7,8},{8,9},{9,10},{10,1... | collective-permute-start | bytes 2752520 | tf_op jit(solution)/shard_map/ppermute | solution.py:183
  61.6 40.9 %collective-permute-start.3 = (bf16[7,256,256]{2,1,0:T(8,128)(2,1)S(1)}, bf16[7,256,256]{2,1,0:T(8,128)(2,1)S(1)}, u32[]{:S(2)}, u32[]{:S(2)}) collective-permute-start(bf16[7,256,256]{2,1,0:T(8,128)(2,1)S(1)} %collective-permute-done.1), channel_id=1, source_target_pairs={{0,15},{1,0},{2,1},{3,2},{4,3},{5,4},{6,5},{7,6},{8,7},{9,8},{10,9... | collective-permute-start | bytes 2752520 | tf_op jit(solution)/shard_map/ppermute | solution.py:188
  100.1 40.0 %collective-permute-start.4 = (bf16[7,256,256]{2,1,0:T(8,128)(2,1)S(1)}, bf16[7,256,256]{2,1,0:T(8,128)(2,1)S(1)}, u32[]{:S(2)}, u32[]{:S(2)}) collective-permute-start(bf16[7,256,256]{2,1,0:T(8,128)(2,1)S(1)} %collective-permute-done.2), channel_id=1, source_target_pairs={{0,1},{1,2},{2,3},{3,4},{4,5},{5,6},{6,7},{7,8},{8,9},{9,10},{10,1... | collective-permute-start | bytes 2752520 | tf_op jit(solution)/shard_map/ppermute | solution.py:183
  102.5 40.0 %collective-permute-start.5 = (bf16[7,256,256]{2,1,0:T(8,128)(2,1)S(1)}, bf16[7,256,256]{2,1,0:T(8,128)(2,1)}, u32[]{:S(2)}, u32[]{:S(2)}) collective-permute-start(bf16[7,256,256]{2,1,0:T(8,128)(2,1)S(1)} %collective-permute-done.3), channel_id=1, source_target_pairs={{0,15},{1,0},{2,1},{3,2},{4,3},{5,4},{6,5},{7,6},{8,7},{9,8},{10,9... | collective-permute-start | bytes 2752520 | tf_op jit(solution)/shard_map/ppermute | solution.py:188
  140.1 39.9 %collective-permute-start.6 = (bf16[7,256,256]{2,1,0:T(8,128)(2,1)S(1)}, bf16[7,256,256]{2,1,0:T(8,128)(2,1)}, u32[]{:S(2)}, u32[]{:S(2)}) collective-permute-start(bf16[7,256,256]{2,1,0:T(8,128)(2,1)S(1)} %collective-permute-done.4), channel_id=1, source_target_pairs={{0,1},{1,2},{2,3},{3,4},{4,5},{5,6},{6,7},{7,8},{8,9},{9,10},{10,1... | collective-permute-start | bytes 2752520 | tf_op jit(solution)/shard_map/ppermute | solution.py:183
  142.6 40.8 %collective-permute-start.7 = (bf16[7,256,256]{2,1,0:T(8,128)(2,1)}, bf16[7,256,256]{2,1,0:T(8,128)(2,1)}, u32[]{:S(2)}, u32[]{:S(2)}) collective-permute-start(bf16[7,256,256]{2,1,0:T(8,128)(2,1)} %collective-permute-done.5), channel_id=1, source_target_pairs={{0,15},{1,0},{2,1},{3,2},{4,3},{5,4},{6,5},{7,6},{8,7},{9,8},{10,9... | collective-permute-start | bytes 2752520 | tf_op jit(solution)/shard_map/ppermute | solution.py:188
  180.0 40.3 %collective-permute-start.8 = (bf16[7,256,256]{2,1,0:T(8,128)(2,1)}, bf16[7,256,256]{2,1,0:T(8,128)(2,1)}, u32[]{:S(2)}, u32[]{:S(2)}) collective-permute-start(bf16[7,256,256]{2,1,0:T(8,128)(2,1)} %collective-permute-done.6), channel_id=1, source_target_pairs={{0,1},{1,2},{2,3},{3,4},{4,5},{5,6},{6,7},{7,8},{8,9},{9,10},{10,1... | collective-permute-start | bytes 2752520 | tf_op jit(solution)/shard_map/ppermute | solution.py:183
  183.4 42.8 %collective-permute-start.9 = (bf16[7,256,256]{2,1,0:T(8,128)(2,1)}, bf16[7,256,256]{2,1,0:T(8,128)(2,1)}, u32[]{:S(2)}, u32[]{:S(2)}) collective-permute-start(bf16[7,256,256]{2,1,0:T(8,128)(2,1)} %collective-permute-done.7), channel_id=1, source_target_pairs={{0,15},{1,0},{2,1},{3,2},{4,3},{5,4},{6,5},{7,6},{8,7},{9,8},{10,9... | collective-permute-start | bytes 2752520 | tf_op jit(solution)/shard_map/ppermute | solution.py:188
  220.3 24.8 %collective-permute-start.10 = (bf16[7,256,256]{2,1,0:T(8,128)(2,1)}, bf16[7,256,256]{2,1,0:T(8,128)(2,1)}, u32[]{:S(2)}, u32[]{:S(2)}) collective-permute-start(bf16[7,256,256]{2,1,0:T(8,128)(2,1)} %collective-permute-done.8), channel_id=1, source_target_pairs={{0,1},{1,2},{2,3},{3,4},{4,5},{5,6},{6,7},{7,8},{8,9},{9,10},{10,1... | collective-permute-start | bytes 2752520 | tf_op jit(solution)/shard_map/ppermute | solution.py:183
  226.2 37.7 %collective-permute-start.11 = (bf16[7,256,256]{2,1,0:T(8,128)(2,1)}, bf16[7,256,256]{2,1,0:T(8,128)(2,1)S(1)}, u32[]{:S(2)}, u32[]{:S(2)}) collective-permute-start(bf16[7,256,256]{2,1,0:T(8,128)(2,1)} %collective-permute-done.9), channel_id=1, source_target_pairs={{0,15},{1,0},{2,1},{3,2},{4,3},{5,4},{6,5},{7,6},{8,7},{9,8},{10,9... | collective-permute-start | bytes 2752520 | tf_op jit(solution)/shard_map/ppermute | solution.py:188
  245.1 42.0 %collective-permute-start.12 = (bf16[7,256,256]{2,1,0:T(8,128)(2,1)}, bf16[7,256,256]{2,1,0:T(8,128)(2,1)S(1)}, u32[]{:S(2)}, u32[]{:S(2)}) collective-permute-start(bf16[7,256,256]{2,1,0:T(8,128)(2,1)} %collective-permute-done.10), channel_id=1, source_target_pairs={{0,1},{1,2},{2,3},{3,4},{4,5},{5,6},{6,7},{7,8},{8,9},{9,10},{10,1... | collective-permute-start | bytes 2752520 | tf_op jit(solution)/shard_map/ppermute | solution.py:183
  263.9 36.6 %collective-permute-start.13 = (bf16[7,256,256]{2,1,0:T(8,128)(2,1)S(1)}, bf16[7,256,256]{2,1,0:T(8,128)(2,1)S(1)}, u32[]{:S(2)}, u32[]{:S(2)}) collective-permute-start(bf16[7,256,256]{2,1,0:T(8,128)(2,1)S(1)} %collective-permute-done.11), channel_id=1, source_target_pairs={{0,15},{1,0},{2,1},{3,2},{4,3},{5,4},{6,5},{7,6},{8,7},{9,8},{10,9... | collective-permute-start | bytes 2752520 | tf_op jit(solution)/shard_map/ppermute | solution.py:188
  287.1 30.7 %collective-permute-start.14 = (bf16[7,256,256]{2,1,0:T(8,128)(2,1)S(1)}, bf16[7,256,256]{2,1,0:T(8,128)(2,1)S(1)}, u32[]{:S(2)}, u32[]{:S(2)}) collective-permute-start(bf16[7,256,256]{2,1,0:T(8,128)(2,1)S(1)} %collective-permute-done.12), channel_id=1, source_target_pairs={{0,1},{1,2},{2,3},{3,4},{4,5},{5,6},{6,7},{7,8},{8,9},{9,10},{10,1... | collective-permute-start | bytes 2752520 | tf_op jit(solution)/shard_map/ppermute | solution.py:183
  502.9 1.2 collective-permute-start.15
  504.6 2.4 collective-permute-start.16
  949.1 643.1 %all-reduce.2.cloned.1.call-start = ((), (), s32[]{:S(2)}) async-start(), calls=%async_computation.2 | async-start | bytes 1835008 | tf_op jit(solution)/shard_map/psum | solution.py:356
  (98 other events, 717.9 us)
Sparse Core Ops, SparseCore 0:
  949.2 615.1 reduce-scatter.1
  1567.3 24.8 all-reduce.1
